TPU v7x, 32 devices: a whole 2x2x4 slice. The times are simulated.
32 devices in a mesh: kpt: 2 (over y), row: 8 (over z, x), freq: 2 (over core).
Axes of the slice: x: 2, y: 2, z: 4, core: 2. Of those that a mesh axis runs over, the one named last changes fastest.
Arguments:
- screened: bfloat16 [8, 2, 8192, 8192], P(('kpt', 'freq'), None, 'row'), parts along dimension 0, may hold values from -0.0625 to 0.0625
- elements: bfloat16 [2, 1024, 8192], P(None, 'kpt', 'row'), parts along dimension 1, may hold values from -0.59765625 to 0.59765625
- node_freq: float32 [4], P('freq'), may hold values from 0.1 to 2
- node_weight: float32 [4], P('freq'), may hold values from 0.1 to 1
- band_energy: float32 [1024], P('kpt'), parts along dimension 0, may hold values from -1 to 1
- energy_grid: float32 [64], replicated, may hold values from -1 to 1
- pair_state: int32 [1024], P('kpt'), parts along dimension 0, may hold values from 0 to 31
- pair_band: int32 [1024], P('kpt'), parts along dimension 0, may hold values from 0 to 511
Outputs:
- sigma: float32 [2, 64, 64], P(None, 'kpt'), parts along dimension 1
There are 2 independent parts, one for each index of `kpt`. A program takes and returns all parts, laid end to end along the dimension named above; an argument that names none is the same for every part. Nothing has to cross between parts.
All inputs are finite; a program needn't handle non-finite values.
Results may differ from a plain program's by a relative error of at most 0.0003.
Values may be sent and summed in bfloat16 or wider, within the bound.
A program may use at most 192 MiB of HBM per device.

v0:
```python
import jax
import jax.numpy as jnp
from jax import lax
from jax.sharding import PartitionSpec as P

NSTATE = 32


def product(weights, piece):
    return jnp.einsum("jgc,pc->jgp", weights, piece, preferred_element_type=jnp.float32)


def self_energy(
    form_re, form_im, node_freq, node_weight, band_energy, energy_grid, pair_state, pair_band
):
    band_onehot = (
        pair_band[:, None] == jnp.arange(band_energy.shape[0], dtype=jnp.int32)[None, :]
    ).astype(jnp.float32)
    pair_eps = jnp.dot(band_onehot, band_energy, precision=lax.Precision.HIGHEST)
    delta = energy_grid[None, :] - pair_eps[:, None]
    factor = (
        node_weight[:, None, None]
        * delta[None]
        / (delta[None] ** 2 + node_freq[:, None, None] ** 2)
    )
    terms_re = jnp.sum(form_re[:, :, None] * factor, axis=0)
    terms_im = jnp.sum(form_im[:, :, None] * factor, axis=0)
    state_onehot = (jnp.arange(NSTATE, dtype=jnp.int32)[:, None] == pair_state[None, :]).astype(
        jnp.float32
    )
    sig_re = jnp.dot(state_onehot, terms_re, precision=lax.Precision.HIGHEST)
    sig_im = jnp.dot(state_onehot, terms_im, precision=lax.Precision.HIGHEST)
    return jnp.stack([sig_re, sig_im])


def per_device(
    screened, elements, node_freq, node_weight, band_energy, energy_grid, pair_state, pair_band
):
    w_real = screened[:, 0]
    w_imag = screened[:, 1]
    npair = elements.shape[1]
    half = npair // lax.axis_size("freq")
    mine = lax.dynamic_slice_in_dim(elements, lax.axis_index("freq") * half, half, 1)
    collected = lax.all_gather(mine, "row", axis=2, tiled=True)
    piece = lax.all_gather(collected, "freq", axis=1, tiled=True)
    part_real = product(w_real, piece[0]) - product(w_imag, piece[1])
    part_imag = product(w_real, piece[1]) + product(w_imag, piece[0])
    stacked = jnp.stack([part_real, part_imag])
    y_real = stacked[0]
    y_imag = stacked[1]
    own_real = elements[0].T.astype(jnp.float32)[None]
    own_imag = elements[1].T.astype(jnp.float32)[None]
    form_re = jnp.sum(own_real * y_real + own_imag * y_imag, axis=1)
    form_im = jnp.sum(own_real * y_imag - own_imag * y_real, axis=1)
    form_re, form_im = lax.psum((form_re, form_im), "row")
    partial_sigma = self_energy(
        form_re, form_im, node_freq, node_weight, band_energy, energy_grid, pair_state, pair_band
    )
    return lax.psum(partial_sigma, "freq")


def solution(mesh):
    in_specs = (
        P(("kpt", "freq"), None, "row", None),
        P(None, "kpt", "row"),
        P("freq"),
        P("freq"),
        P("kpt"),
        P(),
        P("kpt"),
        P("kpt"),
    )
    out_specs = P(None, "kpt", None)
    return jax.shard_map(
        per_device, mesh=mesh, in_specs=in_specs, out_specs=out_specs, check_vma=False
    )
```

profile of v0, /device:TPU:0, one launch (start us, length us, event | category | flops | bytes accessed | tf_op | source)
XLA Modules:
  0.0 302.2 jit_solution(1204558639361420559)
XLA Ops:
  6.5 0.0 copy-start
  6.5 0.0 copy-start.1
  6.5 0.0 copy-start.10
  6.5 0.0 copy-start.9
  6.5 0.0 copy-start.6
  6.5 0.0 all-gather.3.cloned.1.call-start
  6.6 2.4 constant_dynamic-slice_fusion
  9.0 0.0 all-gather.3.cloned.1.call-update
  9.0 0.0 all-gather.5.cloned.1.call-start
  9.1 127.7 %all-gather.3.cloned.1.call-done = bf16[2,256,8192]{2,1,0:T(8,128)(2,1)} async-done(((bf16[2,256,1024]{2,1,0:T(8,128)(2,1)}), bf16[2,256,8192]{2,1,0:T(8,128)(2,1)}) %all-gather.3.cloned.1.call-update) | async-done | bytes 8388624 | tf_op jit(solution)/shard_map/all_gather | solution.py:44
  136.8 0.0 all-gather.5.cloned.1.call-update
  136.8 0.0 copy-done.10
  136.8 0.5 integer_pow.13
  137.3 0.0 copy-done
  137.3 0.0 copy-done.9
  137.3 0.6 fusion.16
  137.9 0.0 copy-done.6
  137.9 0.8 broadcast_subtract_fusion
  138.7 0.0 copy-done.1
  138.7 2.5 convert_bitcast_fusion.1
  141.2 25.4 %all-gather.5.cloned.1.call-done = bf16[2,512,8192]{2,1,0:T(8,128)(2,1)} async-done(((bf16[2,256,8192]{2,1,0:T(8,128)(2,1)}), bf16[2,512,8192]{2,1,0:T(8,128)(2,1)}) %all-gather.5.cloned.1.call-update) | async-done | bytes 16777232 | tf_op jit(solution)/shard_map/all_gather | solution.py:45
  166.6 24.9 %fusion = f32[512,2,1024]{2,0,1:T(8,128)} fusion(bf16[2,2,1024,8192]{3,2,1,0:T(8,128)(2,1)} %param.8, bf16[2,512,8192]{2,1,0:T(8,128)(2,1)} %all-gather.5.cloned.1.call-done), kind=kOutput, calls=%fused_computation | convolution fusion | flops 17179869184 | bytes 46137344 | tf_op jit(solution)/shard_map/jgc,pc->jgp/dot_general | solution.py:10
  191.5 24.9 %fusion.2 = f32[512,2,1024]{2,0,1:T(8,128)} fusion(bf16[2,2,1024,8192]{3,2,1,0:T(8,128)(2,1)} %param.8, bf16[2,512,8192]{2,1,0:T(8,128)(2,1)} %all-gather.5.cloned.1.call-done), kind=kOutput, calls=%fused_computation.2 | convolution fusion | flops 17179869184 | bytes 46137344 | tf_op jit(solution)/shard_map/jgc,pc->jgp/dot_general | solution.py:10
  216.5 0.0 copy-start.2
  216.5 25.1 %fusion.6 = f32[512,2,1024]{2,0,1:T(8,128)} fusion(bf16[2,2,1024,8192]{3,2,1,0:T(8,128)(2,1)} %param.8, bf16[2,512,8192]{2,1,0:T(8,128)(2,1)} %all-gather.5.cloned.1.call-done), kind=kOutput, calls=%fused_computation.6 | convolution fusion | flops 17179869184 | bytes 46137344 | tf_op jit(solution)/shard_map/jgc,pc->jgp/dot_general | solution.py:10
  241.5 0.0 copy-done.2
  241.5 0.0 copy-start.3
  241.6 0.0 copy-start.4
  241.6 0.0 copy-start.7
  241.6 0.0 copy-start.8
  241.6 0.0 copy-start.5
  241.6 27.3 %fusion.13 = (f32[2,512]{1,0:T(2,128)S(1)}, f32[2,512]{1,0:T(2,128)S(1)}) fusion(f32[1024,512]{0,1:T(8,128)} %get-tuple-element.12, f32[1024,512]{0,1:T(8,128)S(1)} %copy-done.2, f32[512,2,1024]{2,0,1:T(8,128)} %fusion, f32[512,2,1024]{2,0,1:T(8,128)} %fusion.6, f32[512,2,1024]{2,0,1:T(8,128)} %fusion.2, bf16[2,2,1024,8192]{3,2,1,0:T(8,128)(2,1)} %param.8, ...), kind=kOutput, calls=%fused_computation.17 | convolution fusion | flops 17190354944 | bytes 58728448 | tf_op jit(solution)/shard_map/jgc,pc->jgp/dot_general | solution.py:10
  268.9 21.9 %all-reduce = (f32[2,512]{1,0:T(2,128)S(1)}, f32[2,512]{1,0:T(2,128)S(1)}) all-reduce(f32[2,512]{1,0:T(2,128)S(1)} %get-tuple-element.5, f32[2,512]{1,0:T(2,128)S(1)} %get-tuple-element.6), channel_id=1, replica_groups=mesh['kpt'=2,'row'=8,'freq'=2] {'row'}, use_global_device_ids=true, to_apply=%region_1.0 | all-reduce | flops 2048 | bytes 16384 | tf_op jit(solution)/shard_map/psum | solution.py:55
  290.8 0.0 copy-done.3
  290.8 0.0 copy-done.4
  290.8 0.0 copy-done.7
  290.8 0.0 copy-done.8
  290.8 0.1 multiply_reduce_fusion.1
  291.0 0.0 copy-done.5
  291.0 0.2 convolution_bitcast_fusion
  291.2 0.2 convolution_bitcast_fusion.1
  291.4 4.0 %psum.23 = f32[2,32,64]{2,1,0:T(8,128)} all-reduce(f32[2,32,64]{2,1,0:T(8,128)S(1)} %pad_maximum_fusion), channel_id=1, replica_groups=mesh['kpt'=2,'row'=8,'freq'=2] {'freq'}, use_global_device_ids=true, to_apply=%region_6.0 | all-reduce | flops 4096 | bytes 32768 | tf_op jit(solution)/shard_map/psum | solution.py:59
  (1 shorter events, 0.0 us)
Async XLA Ops:
  6.5 130.8 %copy-start = (f32[512]{0:T(512)S(1)}, f32[512]{0:T(512)}, u32[]{:S(2)}) copy-start(f32[512]{0:T(512)} %param.12) | copy-start | bytes 6148
  6.5 132.2 %copy-start.1 = (bf16[2,512,1024]{2,1,0:T(8,128)(2,1)S(1)}, bf16[2,512,1024]{2,1,0:T(8,128)(2,1)}, u32[]{:S(2)}) copy-start(bf16[2,512,1024]{2,1,0:T(8,128)(2,1)} %param.9) | copy-start | bytes 6291460
  6.5 130.2 %copy-start.10 = (f32[2]{0:T(128)S(1)}, f32[2]{0:T(128)}, u32[]{:S(2)}) copy-start(f32[2]{0:T(128)} %param.10) | copy-start | bytes 28
  6.5 130.8 %copy-start.9 = (s32[512]{0:T(512)S(1)}, s32[512]{0:T(512)}, u32[]{:S(2)}) copy-start(s32[512]{0:T(512)} %param.15) | copy-start | bytes 6148
  6.5 131.4 %copy-start.6 = (f32[64]{0:T(128)S(1)}, f32[64]{0:T(128)}, u32[]{:S(2)}) copy-start(f32[64]{0:T(128)} %param.13) | copy-start | bytes 772
  6.5 130.2 %all-gather.3.cloned.1.call-start = ((), (), s32[]{:S(2)}) async-start(), calls=%async_computation | async-start | bytes 9437184 | tf_op jit(solution)/shard_map/all_gather | solution.py:44
  9.0 157.6 %all-gather.5.cloned.1.call-start = ((), (), s32[]{:S(2)}) async-start(), calls=%async_computation.1 | async-start | bytes 25165824 | tf_op jit(solution)/shard_map/all_gather | solution.py:45
  216.5 25.1 %copy-start.2 = (f32[1024,512]{0,1:T(8,128)S(1)}, f32[1024,512]{0,1:T(8,128)}, u32[]{:S(2)}) copy-start(f32[1024,512]{0,1:T(8,128)} %get-tuple-element.11) | copy-start | bytes 6291460
  241.5 49.2 %copy-start.3 = (f32[512,64]{0,1:T(8,128)S(1)}, f32[512,64]{0,1:T(8,128)}, u32[]{:S(2)}) copy-start(f32[512,64]{0,1:T(8,128)} %get-tuple-element.13) | copy-start | bytes 393220
  241.6 49.2 %copy-start.4 = (f32[512,64]{0,1:T(8,128)S(1)}, f32[512,64]{0,1:T(8,128)}, u32[]{:S(2)}) copy-start(f32[512,64]{0,1:T(8,128)} %get-tuple-element.14) | copy-start | bytes 393220
  241.6 49.3 %copy-start.7 = (f32[2]{0:T(128)S(1)}, f32[2]{0:T(128)}, u32[]{:S(2)}) copy-start(f32[2]{0:T(128)} %param.11) | copy-start | bytes 28
  241.6 49.3 %copy-start.8 = (f32[2]{0:T(128)S(1)}, f32[2]{0:T(128)}, u32[]{:S(2)}) copy-start(f32[2]{0:T(128)} %integer_pow.13) | copy-start | bytes 28
  241.6 49.4 %copy-start.5 = (s32[512]{0:T(512)S(1)}, s32[512]{0:T(512)}, u32[]{:S(2)}) copy-start(s32[512]{0:T(512)} %param.14) | copy-start | bytes 6148
Sparse Core Ops, SparseCore 0:
  9.5 127.1 all-gather.2
  138.3 28.2 all-gather.4
where the time goes:
time: 302 us
  waiting for transfers between devices  153 us (51%)
  matrix products  103 us (34%)
  blocking collectives  25.9 us (9%)
  between operations  13.5 us (4%)
  other arithmetic  3.93 us (1%)
    all_gather x1, waiting for transfers between devices, per_device(): collected = lax.all_gather(mine, 'row', axis=2, tiled=True)  128 us
    dot_general x4, matrix products, product(): jnp.einsum('jgc,pc->jgp', weights, piece, preferred_element_type=jnp.floa...  102 us
    all_gather x1, waiting for transfers between devices, per_device(): piece = lax.all_gather(collected, 'freq', axis=1, tiled=True)  25.4 us
    psum x1, blocking collectives, per_device(): form_re, form_im = lax.psum((form_re, form_im), 'row')  21.9 us
  transfers between devices with their start and end apart: 2, of which 2 were waited for; matrix products, arithmetic and copies ran while one was open for 1% of the time, Pallas kernels for 0%

commit v1 on v0

--- a/solution.py
+++ b/solution.py
@@ -1,9 +1,14 @@
+import functools
+
 import jax
 import jax.numpy as jnp
 from jax import lax
+from jax.experimental import pallas as pl
+from jax.experimental.pallas import tpu as pltpu
 from jax.sharding import PartitionSpec as P
 
 NSTATE = 32
+TILE = 512
 
 
 def product(weights, piece):
@@ -33,9 +38,205 @@
     return jnp.stack([sig_re, sig_im])
 
 
+def ring_position(idx, n):
+    par = idx % 2
+    return (1 - par) * (idx // 2) + par * (n - 1 - idx // 2)
+
+
+def ring_index(pos, n):
+    high = pos // (n // 2)
+    return (1 - high) * (2 * pos) + high * (2 * (n - 1 - pos) + 1)
+
+
+def ring_kernel(
+    n, nodes, rows, chunk, wide, tile, depth,
+    w_hbm, m_hbm, out_ref,
+    held, wbuf, rhs, own_sem, w_sem, send_sem, recv_sem, sib_send, sib_recv,
+):
+    me = lax.axis_index("row")
+    core = lax.axis_index("freq")
+    pos = ring_position(me, n)
+    right = ring_index((pos + 1) % n, n)
+    left = ring_index((pos + n - 1) % n, n)
+    other = 1 - core
+    half = wide // 2
+    units = 2 * n
+
+    def item(step, way):
+        hop = (step + 1) // 2
+        first = (step + 1) % 2
+        owner_pos = (pos + n + (2 * way - 1) * hop) % n
+        part = (1 - way) * first + way * (1 - first)
+        return ring_index(owner_pos, n), part
+
+    def w_copies(unit):
+        owner, part = item(unit // 2, unit % 2)
+        slot = unit % depth
+        start = pl.multiple_of(owner * 2 * chunk + part * chunk, 128)
+        return [
+            pltpu.make_async_copy(
+                w_hbm.at[j, c, :, pl.ds(start, chunk)],
+                wbuf.at[slot, j, :, pl.ds(c * chunk, chunk)],
+                w_sem.at[slot, j, c],
+            )
+            for j in range(nodes)
+            for c in range(2)
+        ]
+
+    def send(step, way, owner, part):
+        ref = held.at[owner, part, core]
+        return pltpu.make_async_remote_copy(
+            src_ref=ref,
+            dst_ref=ref,
+            send_sem=send_sem.at[step, way],
+            recv_sem=recv_sem.at[step, way],
+            device_id={"row": right if way == 0 else left},
+            device_id_type=pl.DeviceIdType.MESH,
+        )
+
+    def pass_over(step, way, owner, part, core_of):
+        ref = held.at[owner, part, core_of]
+        return pltpu.make_async_remote_copy(
+            src_ref=ref,
+            dst_ref=ref,
+            send_sem=sib_send.at[step, way],
+            recv_sem=sib_recv.at[step, way],
+            device_id={"freq": other},
+            device_id_type=pl.DeviceIdType.MESH,
+        )
+
+    own = pltpu.make_async_copy(m_hbm, held.at[me], own_sem)
+    own.start()
+    for unit in range(depth - 1):
+        for copy in w_copies(unit):
+            copy.start()
+    barrier = pltpu.get_barrier_semaphore()
+    pl.semaphore_signal(barrier, device_id={"row": right}, device_id_type=pl.DeviceIdType.MESH)
+    pl.semaphore_signal(barrier, device_id={"row": left}, device_id_type=pl.DeviceIdType.MESH)
+    pl.semaphore_signal(barrier, device_id={"freq": other}, device_id_type=pl.DeviceIdType.MESH)
+    own.wait()
+    pl.semaphore_wait(barrier, 3)
+    for step in (1, 2):
+        for way in (0, 1):
+            part = (step + 1) % 2 if way == 0 else 1 - (step + 1) % 2
+            send(step, way, me, part).start()
+    out_ref[...] = jnp.zeros_like(out_ref)
+
+    def compute(unit):
+        slot = unit % depth
+        owner, part = item(unit // 2, unit % 2)
+        for f in range(2):
+            rhs[f, :chunk, :] = held[owner, part, f]
+            rhs[f, chunk:, :half] = -held[owner, part, f, :, half:]
+            rhs[f, chunk:, half:] = held[owner, part, f, :, :half]
+        for copy in w_copies(unit):
+            copy.wait()
+
+        @pl.when(unit + depth - 1 < units)
+        def _():
+            for copy in w_copies(unit + depth - 1):
+                copy.start()
+
+        tiles = rows // tile
+
+        def one(i, carry):
+            j = i // (2 * tiles)
+            f = (i // tiles) % 2
+            t = i % tiles
+            spot = pl.ds(pl.multiple_of(t * tile, tile), tile)
+            y = jnp.dot(wbuf[slot, j, spot, :], rhs[f], preferred_element_type=jnp.float32)
+            per = chunk // tile
+            mine = pl.ds(pl.multiple_of((t % per) * tile, tile), tile)
+            m = held[me, t // per, f, mine, :].astype(jnp.float32)
+            r, s = m[:, :half], m[:, half:]
+            yr, yi = y[:, :half], y[:, half:]
+            out_ref[0, j, f] += jnp.sum((r * yr + s * yi).reshape(tile // 8, 8, half), axis=0)
+            out_ref[1, j, f] += jnp.sum((r * yi - s * yr).reshape(tile // 8, 8, half), axis=0)
+            return carry
+
+        lax.fori_loop(0, nodes * 2 * tiles, one, 0)
+
+    def step_body(step, carry):
+        @pl.when(step >= 1)
+        def _():
+            for way in (0, 1):
+                owner, part = item(step, way)
+                send(step, way, owner, part).wait_recv()
+
+                @pl.when(step + 2 < n)
+                def _():
+                    send(step + 2, way, owner, part).start()
+
+                pass_over(step, way, owner, part, core).start()
+            for way in (0, 1):
+                owner, part = item(step, way)
+                pass_over(step, way, owner, part, other).wait_recv()
+
+        def each(way, c):
+            compute(2 * step + way)
+            return c
+
+        lax.fori_loop(0, 2, each, 0)
+        return carry
+
+    lax.fori_loop(0, n, step_body, 0)
+
+    def drain(step, carry):
+        for way in (0, 1):
+            owner, part = item(step, way)
+            send(step, way, owner, part).wait_send()
+            pass_over(step, way, owner, part, core).wait_send()
+        return carry
+
+    lax.fori_loop(1, n, drain, 0)
+
+
+def ring_forms(screened, elements):
+    nodes, _, rows, ng = screened.shape
+    n = lax.axis_size("row")
+    npair = elements.shape[1]
+    block = elements.shape[2]
+    chunk = block // 2
+    wide = npair
+    tile = min(TILE, chunk)
+    depth = 4
+    m = elements.reshape(2, 2, npair // 2, 2, chunk).transpose(3, 1, 4, 0, 2)
+    m = m.reshape(2, 2, chunk, wide)
+    out = pl.pallas_call(
+        functools.partial(ring_kernel, n, nodes, rows, chunk, wide, tile, depth),
+        out_shape=jax.ShapeDtypeStruct((2, nodes, 2, 8, npair // 2), jnp.float32),
+        in_specs=[pl.BlockSpec(memory_space=pl.ANY)] * 2,
+        out_specs=pl.BlockSpec(memory_space=pltpu.VMEM),
+        scratch_shapes=[
+            pltpu.VMEM((n, 2, 2, chunk, wide), jnp.bfloat16),
+            pltpu.VMEM((depth, nodes, rows, 2 * chunk), jnp.bfloat16),
+            pltpu.VMEM((2, 2 * chunk, wide), jnp.bfloat16),
+            pltpu.SemaphoreType.DMA,
+            pltpu.SemaphoreType.DMA((depth, nodes, 2)),
+            pltpu.SemaphoreType.DMA((n, 2)),
+            pltpu.SemaphoreType.DMA((n, 2)),
+            pltpu.SemaphoreType.DMA((n, 2)),
+            pltpu.SemaphoreType.DMA((n, 2)),
+        ],
+        compiler_params=pltpu.CompilerParams(
+            collective_id=0, has_side_effects=True, vmem_limit_bytes=60 * 1024 * 1024
+        ),
+    )(screened, m)
+    forms = jnp.sum(out, axis=3).reshape(2, nodes, npair)
+    return forms[0], forms[1]
+
+
 def per_device(
     screened, elements, node_freq, node_weight, band_energy, energy_grid, pair_state, pair_band
 ):
+    n = lax.axis_size("row")
+    if n >= 4 and n % 2 == 0 and elements.shape[2] % 256 == 0 and elements.shape[1] % 256 == 0:
+        form_re, form_im = ring_forms(screened, elements)
+        partial_sigma = self_energy(
+            form_re, form_im, node_freq, node_weight, band_energy, energy_grid, pair_state,
+            pair_band,
+        )
+        return lax.psum(partial_sigma, ("row", "freq"))
     w_real = screened[:, 0]
     w_imag = screened[:, 1]
     npair = elements.shape[1]

time: 302 us -> 205 us (0.68)
  waiting for transfers between devices: 153 us -> 0 us
  Pallas kernels: 0 us -> 122 us
  matrix products: 103 us -> 1.02 us
  blocking collectives: 25.9 us -> 63.4 us
  local copies, waits for them, and re-layouts: 2.45 us -> 16.6 us
  between operations: 13.5 us -> 0.14 us
    all_gather x2 -> x0, waiting for transfers between devices: 153 us -> none  [the longest x1 128 us: per_device(): collected = lax.all_gather(mine, 'row', axis=2, tiled=True)]
    pallas_call x0 -> x1, Pallas kernels: none -> 122 us  [ring_forms(): pl.pallas_call(functools.partial(ring_kernel, n, nodes, rows, chunk, wide...]
    dot_general x4 -> x0, matrix products: 102 us -> none  [product(): jnp.einsum('jgc,pc->jgp', weights, piece, preferred_element_type=jnp.floa...]
    psum x2 -> x1, blocking collectives: 25.9 us -> 63.4 us  [per_device(): return lax.psum(partial_sigma, ('row', 'freq'))]
    reshape x0 -> x3, local copies, waits for them, and re-layouts: none -> 16.6 us  [the longest x2 13.9 us: ring_forms(): m = elements.reshape(2, 2, npair // 2, 2, chunk).transpose(3, 1, 4, 0, 2)]
  transfers between devices with their start and end apart: 2 -> 0, of which waited for: 2 -> 0; matrix products, arithmetic and copies ran while one was open for 1% -> 0% of each run, Pallas kernels for 0% -> 0%
where the time goes in v1:
time: 205 us; the launch traced here: 204 us
  Pallas kernels  122 us (60%)
  blocking collectives  63.4 us (31%)
  local copies, waits for them, and re-layouts  16.6 us (8%)
    pallas_call x1, Pallas kernels, ring_forms(): pl.pallas_call(functools.partial(ring_kernel, n, nodes, rows, chunk, wide...  122 us
    psum x1, blocking collectives, per_device(): return lax.psum(partial_sigma, ('row', 'freq'))  63.4 us
    reshape x2, local copies, waits for them, and re-layouts, ring_forms(): m = elements.reshape(2, 2, npair // 2, 2, chunk).transpose(3, 1, 4, 0, 2)  13.9 us

profile of v1, /device:TPU:0, one launch (start us, length us, event | category | flops | bytes accessed | tf_op | source)
XLA Modules:
  0.0 204.5 jit_solution(10316786641856236783)
XLA Ops:
  0.0 0.0 copy-start
  0.0 4.5 %reshape.69 = bf16[2,2,256,2,512]{4,3,2,1,0:T(2,128)(2,1)} reshape(bf16[2,512,1024]{2,1,0:T(8,128)(2,1)} %param.9) | data formatting | bytes 4194304 | tf_op jit(solution)/shard_map/reshape | solution.py:203
  4.5 9.4 %copy.10 = bf16[2,2,256,2,512]{2,0,4,1,3:T(2,128)(2,1)S(1)} copy(bf16[2,2,256,2,512]{4,3,2,1,0:T(2,128)(2,1)} %reshape.69) | data formatting | bytes 4194304 | tf_op jit(solution)/shard_map/reshape | solution.py:203
  13.9 2.6 %reshape.70.m_hbm = bf16[2,2,512,512]{3,2,1,0:T(8,128)(2,1)} reshape(bf16[2,2,512,2,256]{4,3,2,1,0:T(2,128)(2,1)S(1)} %bitcast.19) | data formatting | bytes 4194304 | tf_op jit(solution)/shard_map/reshape | solution.py:204
  16.6 0.0 copy-start.4
  16.6 0.0 copy-start.2
  16.6 0.0 copy-start.5
  16.6 0.0 copy-start.3
  16.6 0.0 copy-start.1
  16.6 122.2 %shard_map.82 = f32[2,2,2,8,256]{4,3,2,1,0:T(8,128)} custom-call(bf16[2,2,1024,8192]{3,2,1,0:T(8,128)(2,1)} %w_hbm.1, bf16[2,2,512,512]{3,2,1,0:T(8,128)(2,1)} %reshape.70.m_hbm), custom_call_target="tpu_custom_call" | custom-call | tf_op jit(solution)/shard_map/pallas_call | solution.py:205
  138.8 0.9 reduce_sum.27
  139.7 0.0 copy-done
  139.7 0.0 copy-done.4
  139.8 0.6 fusion
  140.4 0.0 copy-done.2
  140.4 0.1 broadcast_subtract_fusion
  140.5 0.0 copy-done.5
  140.5 0.0 copy-done.3
  140.5 0.1 multiply_reduce_fusion.1
  140.7 0.0 copy-done.1
  140.7 0.2 convolution_bitcast_fusion
  140.9 0.2 convolution_bitcast_fusion.1
  141.1 63.4 %psum.7 = f32[2,32,64]{2,1,0:T(8,128)} all-reduce(f32[2,32,64]{2,1,0:T(8,128)S(1)} %pad_maximum_fusion), channel_id=1, replica_groups=mesh['kpt'=2,'row'=8,'freq'=2] {'row','freq'}, use_global_device_ids=true, to_apply=%region_3.0 | all-reduce | flops 4096 | bytes 32768 | tf_op jit(solution)/shard_map/psum | solution.py:239
  (5 shorter events, 0.0 us)
Async XLA Ops:
  0.0 139.7 %copy-start = (f32[512]{0:T(512)S(1)}, f32[512]{0:T(512)}, u32[]{:S(2)}) copy-start(f32[512]{0:T(512)} %param.12) | copy-start | bytes 6148
  16.6 123.2 %copy-start.4 = (s32[512]{0:T(512)S(1)}, s32[512]{0:T(512)}, u32[]{:S(2)}) copy-start(s32[512]{0:T(512)} %param.15) | copy-start | bytes 6148
  16.6 123.8 %copy-start.2 = (f32[64]{0:T(128)S(1)}, f32[64]{0:T(128)}, u32[]{:S(2)}) copy-start(f32[64]{0:T(128)} %param.13) | copy-start | bytes 772
  16.6 123.9 %copy-start.5 = (f32[2]{0:T(128)S(1)}, f32[2]{0:T(128)}, u32[]{:S(2)}) copy-start(f32[2]{0:T(128)} %param.10) | copy-start | bytes 28
  16.6 123.9 %copy-start.3 = (f32[2]{0:T(128)S(1)}, f32[2]{0:T(128)}, u32[]{:S(2)}) copy-start(f32[2]{0:T(128)} %param.11) | copy-start | bytes 28
  16.6 124.1 %copy-start.1 = (s32[512]{0:T(512)S(1)}, s32[512]{0:T(512)}, u32[]{:S(2)}) copy-start(s32[512]{0:T(512)} %param.14) | copy-start | bytes 6148

commit v2 on v1

--- a/solution.py
+++ b/solution.py
@@ -9,6 +9,7 @@
 
 NSTATE = 32
 TILE = 512
+DEPTH = 4
 
 
 def product(weights, piece):
@@ -50,8 +51,10 @@
 
 def ring_kernel(
     n, nodes, rows, chunk, wide, tile, depth,
-    w_hbm, m_hbm, out_ref,
-    held, wbuf, rhs, own_sem, w_sem, send_sem, recv_sem, sib_send, sib_recv,
+    w_hbm, m_hbm, param_ref, out_ref,
+    block, held, wbuf, rhs, acc, forms, peers, twin,
+    own_sem, w_sem, send_sem, recv_sem, sib_send, sib_recv,
+    form_send, form_recv, twin_send, twin_recv,
 ):
     me = lax.axis_index("row")
     core = lax.axis_index("freq")
@@ -105,22 +108,35 @@
             device_id_type=pl.DeviceIdType.MESH,
         )
 
-    own = pltpu.make_async_copy(m_hbm, held.at[me], own_sem)
+    own = pltpu.make_async_copy(m_hbm, block, own_sem)
     own.start()
     for unit in range(depth - 1):
         for copy in w_copies(unit):
             copy.start()
     barrier = pltpu.get_barrier_semaphore()
-    pl.semaphore_signal(barrier, device_id={"row": right}, device_id_type=pl.DeviceIdType.MESH)
-    pl.semaphore_signal(barrier, device_id={"row": left}, device_id_type=pl.DeviceIdType.MESH)
+    for hop in range(1, n):
+        pl.semaphore_signal(
+            barrier, device_id={"row": (me + hop) % n}, device_id_type=pl.DeviceIdType.MESH
+        )
     pl.semaphore_signal(barrier, device_id={"freq": other}, device_id_type=pl.DeviceIdType.MESH)
     own.wait()
-    pl.semaphore_wait(barrier, 3)
+
+    def turn(part, f):
+        pairs = pl.ds(pl.multiple_of(f * half, half), half)
+        for c in range(2):
+            piece = block[c, pairs, part * chunk : (part + 1) * chunk]
+            held[me, part, f, :, c * half : (c + 1) * half] = piece.T
+
+    turn(0, core)
+    turn(1, core)
+    pl.semaphore_wait(barrier, n)
     for step in (1, 2):
         for way in (0, 1):
             part = (step + 1) % 2 if way == 0 else 1 - (step + 1) % 2
             send(step, way, me, part).start()
-    out_ref[...] = jnp.zeros_like(out_ref)
+    turn(0, other)
+    turn(1, other)
+    acc[...] = jnp.zeros_like(acc)
 
     def compute(unit):
         slot = unit % depth
@@ -150,8 +166,8 @@
             m = held[me, t // per, f, mine, :].astype(jnp.float32)
             r, s = m[:, :half], m[:, half:]
             yr, yi = y[:, :half], y[:, half:]
-            out_ref[0, j, f] += jnp.sum((r * yr + s * yi).reshape(tile // 8, 8, half), axis=0)
-            out_ref[1, j, f] += jnp.sum((r * yi - s * yr).reshape(tile // 8, 8, half), axis=0)
+            acc[0, j, f] += jnp.sum((r * yr + s * yi).reshape(tile // 8, 8, half), axis=0)
+            acc[1, j, f] += jnp.sum((r * yi - s * yr).reshape(tile // 8, 8, half), axis=0)
             return carry
 
         lax.fori_loop(0, nodes * 2 * tiles, one, 0)
@@ -181,6 +197,22 @@
 
     lax.fori_loop(0, n, step_body, 0)
 
+    lines = 2 * nodes * 2
+    forms[:lines, :] = jnp.sum(acc[...], axis=3).reshape(lines, half)
+    forms[lines:, :] = jnp.zeros_like(forms[lines:, :])
+
+    def spread(hop):
+        return pltpu.make_async_remote_copy(
+            src_ref=forms,
+            dst_ref=peers.at[hop - 1],
+            send_sem=form_send.at[hop - 1],
+            recv_sem=form_recv.at[hop - 1],
+            device_id={"row": (me + hop) % n},
+            device_id_type=pl.DeviceIdType.MESH,
+        )
+
+    for hop in range(1, n):
+        spread(hop).start()
     def drain(step, carry):
         for way in (0, 1):
             owner, part = item(step, way)
@@ -189,54 +221,90 @@
         return carry
 
     lax.fori_loop(1, n, drain, 0)
-
-
-def ring_forms(screened, elements):
+    total = forms[...]
+    for hop in range(1, n):
+        spread(hop).wait()
+        total += peers[hop - 1]
+    twin[0, :lines, :] = total[:lines, :]
+    twin[0, lines:, :] = param_ref[...]
+    swap = pltpu.make_async_remote_copy(
+        src_ref=twin.at[0],
+        dst_ref=twin.at[1],
+        send_sem=twin_send,
+        recv_sem=twin_recv,
+        device_id={"freq": other},
+        device_id_type=pl.DeviceIdType.MESH,
+    )
+    swap.start()
+    out_ref[0] = twin[0]
+    swap.wait()
+    out_ref[1] = twin[1]
+
+
+def ring_forms(screened, elements, node_freq, node_weight):
     nodes, _, rows, ng = screened.shape
     n = lax.axis_size("row")
     npair = elements.shape[1]
     block = elements.shape[2]
     chunk = block // 2
-    wide = npair
+    half = npair // 2
     tile = min(TILE, chunk)
-    depth = 4
-    m = elements.reshape(2, 2, npair // 2, 2, chunk).transpose(3, 1, 4, 0, 2)
-    m = m.reshape(2, 2, chunk, wide)
+    depth = DEPTH
+    lines = 2 * nodes * 2
+    spare = -(-2 * nodes // 8) * 8
+    params = jnp.concatenate([node_freq, node_weight])
+    params = jnp.pad(params, (0, spare - 2 * nodes))
+    params = jnp.broadcast_to(params[:, None], (spare, half))
     out = pl.pallas_call(
-        functools.partial(ring_kernel, n, nodes, rows, chunk, wide, tile, depth),
-        out_shape=jax.ShapeDtypeStruct((2, nodes, 2, 8, npair // 2), jnp.float32),
-        in_specs=[pl.BlockSpec(memory_space=pl.ANY)] * 2,
+        functools.partial(ring_kernel, n, nodes, rows, chunk, npair, tile, depth),
+        out_shape=jax.ShapeDtypeStruct((2, lines + spare, half), jnp.float32),
+        in_specs=[
+            pl.BlockSpec(memory_space=pl.ANY),
+            pl.BlockSpec(memory_space=pl.ANY),
+            pl.BlockSpec(memory_space=pltpu.VMEM),
+        ],
         out_specs=pl.BlockSpec(memory_space=pltpu.VMEM),
         scratch_shapes=[
-            pltpu.VMEM((n, 2, 2, chunk, wide), jnp.bfloat16),
+            pltpu.VMEM((2, npair, block), jnp.bfloat16),
+            pltpu.VMEM((n, 2, 2, chunk, npair), jnp.bfloat16),
             pltpu.VMEM((depth, nodes, rows, 2 * chunk), jnp.bfloat16),
-            pltpu.VMEM((2, 2 * chunk, wide), jnp.bfloat16),
+            pltpu.VMEM((2, 2 * chunk, npair), jnp.bfloat16),
+            pltpu.VMEM((2, nodes, 2, 8, half), jnp.float32),
+            pltpu.VMEM((lines + spare, half), jnp.float32),
+            pltpu.VMEM((n - 1, lines + spare, half), jnp.float32),
+            pltpu.VMEM((2, lines + spare, half), jnp.float32),
             pltpu.SemaphoreType.DMA,
             pltpu.SemaphoreType.DMA((depth, nodes, 2)),
             pltpu.SemaphoreType.DMA((n, 2)),
             pltpu.SemaphoreType.DMA((n, 2)),
             pltpu.SemaphoreType.DMA((n, 2)),
             pltpu.SemaphoreType.DMA((n, 2)),
+            pltpu.SemaphoreType.DMA((n - 1,)),
+            pltpu.SemaphoreType.DMA((n - 1,)),
+            pltpu.SemaphoreType.DMA,
+            pltpu.SemaphoreType.DMA,
         ],
         compiler_params=pltpu.CompilerParams(
-            collective_id=0, has_side_effects=True, vmem_limit_bytes=60 * 1024 * 1024
+            collective_id=0, has_side_effects=True, vmem_limit_bytes=62 * 1024 * 1024
         ),
-    )(screened, m)
-    forms = jnp.sum(out, axis=3).reshape(2, nodes, npair)
-    return forms[0], forms[1]
+    )(screened, elements, params)
+    forms = out[:, :lines].reshape(2, 2, nodes, npair).transpose(1, 0, 2, 3)
+    forms = forms.reshape(2, 2 * nodes, npair)
+    freqs = out[:, lines : lines + nodes, 0].reshape(-1)
+    weights = out[:, lines + nodes : lines + 2 * nodes, 0].reshape(-1)
+    return forms[0], forms[1], freqs, weights
 
 
 def per_device(
     screened, elements, node_freq, node_weight, band_energy, energy_grid, pair_state, pair_band
 ):
     n = lax.axis_size("row")
-    if n >= 4 and n % 2 == 0 and elements.shape[2] % 256 == 0 and elements.shape[1] % 256 == 0:
-        form_re, form_im = ring_forms(screened, elements)
-        partial_sigma = self_energy(
-            form_re, form_im, node_freq, node_weight, band_energy, energy_grid, pair_state,
-            pair_band,
-        )
-        return lax.psum(partial_sigma, ("row", "freq"))
+    two = n >= 4 and n % 2 == 0 and lax.axis_size("freq") == 2
+    if two and elements.shape[2] % 256 == 0 and elements.shape[1] % 256 == 0:
+        form_re, form_im, freqs, weights = ring_forms(screened, elements, node_freq, node_weight)
+        return self_energy(
+            form_re, form_im, freqs, weights, band_energy, energy_grid, pair_state, pair_band
+        )
     w_real = screened[:, 0]
     w_imag = screened[:, 1]
     npair = elements.shape[1]

time: 205 us -> 138 us (0.67)
  blocking collectives: 63.4 us -> 0 us
  local copies, waits for them, and re-layouts: 16.6 us -> 2.3 us
  Pallas kernels: 122 us -> 131 us
    psum x1 -> x0, blocking collectives: 63.4 us -> none  [per_device(): return lax.psum(partial_sigma, ('row', 'freq'))]
    reshape x3 -> x1, local copies, waits for them, and re-layouts: 16.6 us -> 0.02 us  [ring_forms(): forms = out[:, :lines].reshape(2, 2, nodes, npair).transpose(1, 0, 2, 3)]
    pallas_call x1, Pallas kernels: 122 us -> 131 us  [ring_forms(): pl.pallas_call(functools.partial(ring_kernel, n, nodes, rows, chunk, npai...]
where the time goes in v2:
time: 138 us
  Pallas kernels  131 us (95%)
  other arithmetic  2.52 us (2%)
  local copies, waits for them, and re-layouts  2.3 us (2%)
  matrix products  1.7 us (1%)
    pallas_call x1, Pallas kernels, ring_forms(): pl.pallas_call(functools.partial(ring_kernel, n, nodes, rows, chunk, npai...  131 us

profile of v2, /device:TPU:0, one launch (start us, length us, event | category | flops | bytes accessed | tf_op | source)
XLA Modules:
  0.0 137.6 jit_solution(17883271336009705260)
XLA Ops:
  0.0 0.0 copy-start
  0.0 0.0 copy-start.1
  0.0 0.0 copy-start.2
  0.0 0.7 copy-done
  0.7 0.7 fusion.5
  1.4 1.3 fusion
  2.7 0.7 broadcast_in_dim.2.param_ref
  3.4 131.0 %shard_map.82 = f32[2,16,256]{2,1,0:T(8,128)} custom-call(bf16[2,2,1024,8192]{3,2,1,0:T(8,128)(2,1)} %w_hbm.1, bf16[2,512,1024]{2,1,0:T(8,128)(2,1)} %m_hbm.1, f32[8,256]{1,0:T(8,128)} %broadcast_in_dim.2.param_ref), custom_call_target="tpu_custom_call" | custom-call | tf_op jit(solution)/shard_map/pallas_call | solution.py:258
  134.5 0.9 slice_reduce_fusion
  135.3 0.7 slice.17
  136.1 0.1 mul.37
  136.2 0.1 integer_pow.21
  136.3 0.0 copy-done.2
  136.3 0.1 broadcast_subtract_fusion
  136.4 0.2 multiply_reduce_fusion.1
  136.6 0.0 copy-done.1
  136.6 0.2 convolution_bitcast_fusion.1
  136.8 0.2 convolution_bitcast_fusion
  137.0 0.6 pad_maximum_fusion
  (4 shorter events, 0.1 us)
Async XLA Ops:
  0.0 0.7 copy-start
  0.0 136.6 %copy-start.1 = (s32[512]{0:T(512)S(1)}, s32[512]{0:T(512)}, u32[]{:S(2)}) copy-start(s32[512]{0:T(512)} %param.14) | copy-start | bytes 6148
  0.0 136.3 %copy-start.2 = (f32[64]{0:T(128)S(1)}, f32[64]{0:T(128)}, u32[]{:S(2)}) copy-start(f32[64]{0:T(128)} %param.13) | copy-start | bytes 772

commit v3 on v2

--- a/solution.py
+++ b/solution.py
@@ -170,7 +170,7 @@
             acc[1, j, f] += jnp.sum((r * yi - s * yr).reshape(tile // 8, 8, half), axis=0)
             return carry
 
-        lax.fori_loop(0, nodes * 2 * tiles, one, 0)
+        lax.fori_loop(0, nodes * 2 * tiles, one, 0, unroll=4)
 
     def step_body(step, carry):
         @pl.when(step >= 1)

time: 138 us -> 125 us (0.906)
  Pallas kernels: 131 us -> 118 us
    pallas_call x1, Pallas kernels: 131 us -> 118 us  [ring_forms(): pl.pallas_call(functools.partial(ring_kernel, n, nodes, rows, chunk, npai...]
where the time goes in v3:
time: 125 us
  Pallas kernels  118 us (94%)
  other arithmetic  2.52 us (2%)
  local copies, waits for them, and re-layouts  2.3 us (2%)
  matrix products  1.7 us (1%)
    pallas_call x1, Pallas kernels, ring_forms(): pl.pallas_call(functools.partial(ring_kernel, n, nodes, rows, chunk, npai...  118 us

profile of v3, /device:TPU:0, one launch (start us, length us, event | category | flops | bytes accessed | tf_op | source)
XLA Modules:
  0.0 124.8 jit_solution(7275689429785151946)
XLA Ops:
  0.0 0.0 copy-start
  0.0 0.0 copy-start.1
  0.0 0.0 copy-start.2
  0.0 0.7 copy-done
  0.7 0.7 fusion.5
  1.4 1.3 %fusion = f32[1,512]{1,0:T(1,128)S(1)} fusion(f32[512,1]{0,1:T(1,128)S(1)} %bitcast.14, s32[512]{0:T(512)} %param.15), kind=kOutput, calls=%fused_computation.3 | convolution fusion | flops 3407872 | bytes 6144 | tf_op jit(solution)/shard_map/dot_general | solution.py:25
  2.7 0.7 broadcast_in_dim.2.param_ref
  3.4 118.2 %shard_map.82 = f32[2,16,256]{2,1,0:T(8,128)} custom-call(bf16[2,2,1024,8192]{3,2,1,0:T(8,128)(2,1)} %w_hbm.1, bf16[2,512,1024]{2,1,0:T(8,128)(2,1)} %m_hbm.1, f32[8,256]{1,0:T(8,128)} %broadcast_in_dim.2.param_ref), custom_call_target="tpu_custom_call" | custom-call | tf_op jit(solution)/shard_map/pallas_call | solution.py:258
  121.6 0.9 slice_reduce_fusion
  122.5 0.7 slice.17
  123.2 0.1 mul.37
  123.3 0.1 integer_pow.21
  123.4 0.0 copy-done.2
  123.4 0.1 broadcast_subtract_fusion
  123.5 0.2 multiply_reduce_fusion.1
  123.7 0.0 copy-done.1
  123.7 0.2 convolution_bitcast_fusion.1
  123.9 0.2 convolution_bitcast_fusion
  124.1 0.6 pad_maximum_fusion
  (4 shorter events, 0.1 us)
Async XLA Ops:
  0.0 0.7 copy-start
  0.0 123.7 %copy-start.1 = (s32[512]{0:T(512)S(1)}, s32[512]{0:T(512)}, u32[]{:S(2)}) copy-start(s32[512]{0:T(512)} %param.14) | copy-start | bytes 6148
  0.0 123.4 %copy-start.2 = (f32[64]{0:T(128)S(1)}, f32[64]{0:T(128)}, u32[]{:S(2)}) copy-start(f32[64]{0:T(128)} %param.13) | copy-start | bytes 772
